TPU v7x, 32 devices: a whole 2x2x4 slice. The times are simulated.
32 devices in a mesh: gx: 8 (over z, y), gy: 4 (over x, core).
Axes of the slice: x: 2, y: 2, z: 4, core: 2. Of those that a mesh axis runs over, the one named last changes fastest.
Arguments:
- state: float32 [4, 2, 4194304], P('gy', None, 'gx'), may hold values from -6 to 6
- fields: float32 [22], replicated, may hold values from 0.5 to 2
- couplings: float32 [22], replicated, may hold values from 0.5 to 2
- noise: float32 [4, 4, 2], P('gy'), may hold values from -5 to 5
Outputs:
- final_state: float32 [4, 2, 4194304], P('gy', None, 'gx')
- record: float32 [4, 2], replicated
All inputs are finite; a program needn't handle non-finite values.
Results may differ from a plain program's by a relative error of at most 0.0001.
Values sent between devices are 32-bit elements; how exact they have to be, the bound alone decides.
A program may use at most 128 MiB of HBM per device.

v0:
```python
import jax
import jax.numpy as jnp
from jax import lax
from jax.sharding import PartitionSpec as P

kappa_rate = 4.0
time_step = 0.05


def from_partner(array, axis, bit):
    return lax.ppermute(array, axis, [(i, i ^ 1 << bit) for i in range(lax.axis_size(axis))])


def flip_table(fields, lowest, width):
    row_ids = lax.iota(jnp.int32, 1 << width)
    row_xor = row_ids[:, None] ^ row_ids[None, :]
    table = jnp.zeros((1 << width, 1 << width), jnp.float32)
    for q in range(width):
        table = table + fields[lowest + q] * (row_xor == 1 << q).astype(jnp.float32)
    return table


def block_flip(amplitudes, lowest, width, table):
    shape = amplitudes.shape
    if lowest == 0:
        return jnp.dot(
            amplitudes.reshape(-1, 1 << width),
            table,
            precision=lax.Precision.HIGHEST,
            preferred_element_type=jnp.float32,
        ).reshape(shape)
    viewed = amplitudes.reshape(
        shape[0], shape[1], shape[2] >> lowest + width, 1 << width, 1 << lowest
    )
    result = jnp.einsum(
        "pcakb,kj->pcajb",
        viewed,
        table,
        precision=lax.Precision.HIGHEST,
        preferred_element_type=jnp.float32,
    )
    return result.reshape(shape)


def shards(state, fields, couplings, noise):
    local_len = state.shape[2]
    low_bits = local_len.bit_length() - 1
    group_count = lax.axis_size("gx")
    high_bits = group_count.bit_length() - 1
    count_qubits = low_bits + high_bits
    position = lax.axis_index("gx") * local_len + lax.iota(jnp.int32, local_len)
    first_spin = 1.0 - 2.0 * (position & 1).astype(jnp.float32)
    prior_spin = first_spin
    occupancy = 0.5 * (1.0 - first_spin)
    energy = jnp.zeros((local_len,), jnp.float32)
    for q in range(1, count_qubits):
        spin_now = 1.0 - 2.0 * (position >> q & 1).astype(jnp.float32)
        occupancy = occupancy + 0.5 * (1.0 - spin_now)
        energy = energy + couplings[q - 1] * prior_spin * spin_now
        prior_spin = spin_now
    energy = energy + couplings[count_qubits - 1] * prior_spin * first_spin
    occupancy = occupancy / count_qubits
    block_list = []
    lowest = 0
    while lowest < low_bits:
        width = min(7, low_bits - lowest)
        block_list.append((lowest, width, flip_table(fields, lowest, width)))
        lowest = lowest + width
    amplitudes = state
    half_root = jnp.sqrt(jnp.float32(time_step / 2.0))
    root_kappa = jnp.sqrt(jnp.float32(kappa_rate))
    step_records = []
    for step_id in range(noise.shape[1]):
        result = None
        for apply_lowest, apply_width, table in block_list:
            term = block_flip(amplitudes, apply_lowest, apply_width, table)
            result = term if result is None else result + term
        for b in range(high_bits):
            result = result + fields[low_bits + b] * from_partner(amplitudes, "gx", b)
        weight = amplitudes[:, 0] ** 2 + amplitudes[:, 1] ** 2
        norm_sum, magnet_sum = lax.psum(
            (jnp.sum(weight, axis=1), jnp.sum(weight * occupancy[None, :], axis=1)), "gx"
        )
        magnet = magnet_sum / norm_sum
        factor = jnp.sqrt(local_len * group_count / norm_sum)[:, None]
        shift = occupancy[None, :] - magnet[:, None]
        first = (noise[:, step_id, 0] * half_root)[:, None]
        second = (noise[:, step_id, 1] * half_root)[:, None]
        real_part = amplitudes[:, 0]
        imag_part = amplitudes[:, 1]
        keep = 1.0 - time_step * kappa_rate * 0.5 * shift * shift + time_step * 0.0
        kick = root_kappa * shift
        coherent_real = -result[:, 1] - energy[None, :] * imag_part
        coherent_imag = -result[:, 0] - energy[None, :] * real_part
        new_real = factor * (
            keep * real_part
            + time_step * coherent_real
            + kick * (real_part * first - imag_part * second)
        )
        new_imag = factor * (
            keep * imag_part
            - time_step * coherent_imag
            + kick * (real_part * second + imag_part * first)
        )
        amplitudes = jnp.stack([new_real, new_imag], axis=1)
        drift = root_kappa * magnet * time_step
        local_record = jnp.sum(
            jnp.stack([drift + first[:, 0], drift + second[:, 0]], axis=1), axis=0
        )
        step_records.append(lax.psum(local_record, "gy"))
    record = jnp.stack(step_records)
    return (amplitudes, record)


def solution(mesh):
    placed = (P("gy", None, "gx"), P(), P(), P("gy", None, None))
    return jax.shard_map(
        shards, mesh=mesh, in_specs=placed, out_specs=(P("gy", None, "gx"), P()), check_vma=False
    )
```

profile of v0, /device:TPU:0, one launch (start us, length us, event | category | flops | bytes accessed | tf_op | source)
XLA Modules:
  0.0 1682.6 jit_solution(16624386368531204424)
XLA Ops:
  7.9 91.3 %fusion.159 = (f32[]{:T(128)}, f32[]{:T(128)}) fusion(s32[]{:T(128)S(6)} %mul.5956, f32[1,2,524288]{2,1,0:T(2,128)} %param.4), kind=kLoop, calls=%fused_computation.314 | loop fusion | flops 83886080 | bytes 4194316 | tf_op jit(solution)/shard_map/reduce_sum | solution.py:82
  99.2 102.1 %all-reduce.3 = (f32[1]{0:T(128)}, f32[1]{0:T(128)}) all-reduce(f32[1]{0:T(128)} %bitcast.4, f32[1]{0:T(128)} %bitcast.2), channel_id=1, replica_groups=mesh['gx'=8,'gy'=4] {'gx'}, use_global_device_ids=true, to_apply=%region_3.0 | all-reduce | flops 2 | bytes 16 | tf_op jit(solution)/shard_map/psum | solution.py:81
  201.3 7.7 reshape.2314
  216.4 13.2 convolution_bitcast_fusion.3
  229.6 8.2 reshape.2319
  240.3 9.6 convolution_bitcast_fusion.5
  257.4 12.1 convolution_bitcast_fusion.4
  283.5 12.4 multiply_add_fusion.3
  295.9 145.0 %add_multiply_fusion.10 = (f32[1,1,524288]{2,1,0:T(1,128)S(1)}, f32[1,1,524288]{2,1,0:T(1,128)S(1)}) fusion(f32[]{:T(128)} %bitcast.60, f32[]{:T(128)} %bitcast.59, f32[]{:T(128)} %bitcast.5, s32[]{:T(128)S(6)} %mul.5956, f32[]{:T(128)} %bitcast.3, f32[1,2,524288]{2,1,0:T(2,128)S(1)} %multiply_add_fusion.3, f32[1,2,524288]{2,1,0:T(2,128)S(1)} %copy-done, ...), kind=kLoop, calls=%fused_computation.103 | loop fusion | flops 123731968 | bytes 10485868 | tf_op jit(solution)/shard_map/mul | solution.py:95
  440.9 98.3 %slice_negate_fusion.7 = (f32[1,1,524288]{2,1,0:T(1,128)}, f32[1,1,524288]{2,1,0:T(1,128)S(1)}, f32[1,1,524288]{2,1,0:T(1,128)}, f32[1,1,524288]{2,1,0:T(1,128)}, f32[1,1,524288]{2,1,0:T(1,128)}) fusion(f32[1,2,524288]{2,1,0:T(2,128)S(1)} %multiply_add_fusion.3, f32[]{:T(128)} %bitcast.59, f32[]{:T(128)} %bitcast.60, ...), kind=kLoop, calls=%fused_computation.65 | loop fusion | flops 90177536 | bytes 20971540 | tf_op jit(solution)/shard_map/neg | solution.py:93
  545.1 156.6 %multiply_reduce_fusion.2 = (f32[]{:T(128)}, f32[]{:T(128)}) fusion(s32[]{:T(128)S(6)} %mul.5956, f32[1,2,524288]{2,1,0:T(2,128)S(1)} %multiply_add_fusion.3, f32[]{:T(128)} %bitcast.60, f32[]{:T(128)} %bitcast.59, f32[1,2,524288]{2,1,0:T(2,128)S(1)} %copy-done, f32[]{:T(128)} %bitcast.58, f32[]{:T(128)} %bitcast.57, f32[]{:T(128)} %bitcast.56, ...), kind=kLoop, calls=%fused_computation.131 | loop fusion | flops 133169152 | bytes 8388724 | tf_op jit(solution)/shard_map/reduce_sum | solution.py:82
  701.7 34.1 %all-reduce.2 = (f32[1]{0:T(128)}, f32[1]{0:T(128)}) all-reduce(f32[1]{0:T(128)} %bitcast.62, f32[1]{0:T(128)} %bitcast.64), channel_id=1, replica_groups=mesh['gx'=8,'gy'=4] {'gx'}, use_global_device_ids=true, to_apply=%region_5.0 | all-reduce | flops 2 | bytes 16 | tf_op jit(solution)/shard_map/psum | solution.py:81
  749.6 8.7 convolution_bitcast_fusion.2
  766.0 11.0 fusion.55
  783.8 12.4 fusion.19
  803.1 12.6 multiply_add_fusion.2
  815.7 101.4 %add_multiply_fusion.5 = (f32[1,1,524288]{2,1,0:T(1,128)S(1)}, f32[1,1,524288]{2,1,0:T(1,128)S(1)}, f32[1,1,524288]{2,1,0:T(1,128)S(1)}, f32[1,1,524288]{2,1,0:T(1,128)S(1)}) fusion(f32[1,1,524288]{2,1,0:T(1,128)S(1)} %copy-done.15, f32[1,1,524288]{2,1,0:T(1,128)S(1)} %copy-done.12, f32[1,1,524288]{2,1,0:T(1,128)S(1)} %get-tuple-element.26, f32[]{:T(128)} %bitcast.81, ...), kind=kLoop, calls=%fused_computation.96 | loop fusion | flops 95944704 | bytes 18874388 | tf_op jit(solution)/shard_map/mul | solution.py:95
  923.5 35.1 %multiply_reduce_fusion.1 = (f32[]{:T(128)}, f32[]{:T(128)}, f32[524288]{0:T(1024)}, f32[524288]{0:T(1024)}, f32[524288]{0:T(1024)}) fusion(s32[]{:T(128)S(6)} %mul.5956, f32[]{:T(128)} %bitcast.81, f32[]{:T(128)} %bitcast.80, f32[524288]{0:T(1024)S(1)} %bitcast.344, f32[524288]{0:T(1024)S(1)} %bitcast.341, f32[524288]{0:T(1024)S(1)} %bitcast.340, ...), kind=kLoop, calls=%fused_computation.97 | loop fusion | flops 146276352 | bytes 18874500 | tf_op jit(solution)/shard_map/reduce_sum | solution.py:82
  958.5 154.5 %all-reduce.1 = (f32[1]{0:T(128)}, f32[1]{0:T(128)}) all-reduce(f32[1]{0:T(128)} %bitcast.83, f32[1]{0:T(128)} %bitcast.85), channel_id=1, replica_groups=mesh['gx'=8,'gy'=4] {'gx'}, use_global_device_ids=true, to_apply=%region_9.0 | all-reduce | flops 2 | bytes 16 | tf_op jit(solution)/shard_map/psum | solution.py:81
  1127.0 8.3 convolution_bitcast_fusion.1
  1143.0 11.0 fusion.54
  1160.8 12.4 fusion.18
  1180.0 12.6 multiply_add_fusion.1
  1192.7 101.4 %add_multiply_fusion.3 = (f32[1,1,524288]{2,1,0:T(1,128)S(1)}, f32[1,1,524288]{2,1,0:T(1,128)S(1)}, f32[1,1,524288]{2,1,0:T(1,128)S(1)}, f32[1,1,524288]{2,1,0:T(1,128)S(1)}) fusion(f32[1,1,524288]{2,1,0:T(1,128)S(1)} %copy-done.10, f32[1,1,524288]{2,1,0:T(1,128)S(1)} %copy-done.8, f32[1,1,524288]{2,1,0:T(1,128)S(1)} %get-tuple-element.26, f32[]{:T(128)} %bitcast.97, ...), kind=kLoop, calls=%fused_computation.92 | loop fusion | flops 95944704 | bytes 18874388 | tf_op jit(solution)/shard_map/mul | solution.py:95
  1301.4 13.5 multiply_reduce_fusion
  1314.9 175.0 %all-reduce = (f32[1]{0:T(128)}, f32[1]{0:T(128)}) all-reduce(f32[1]{0:T(128)} %bitcast.99, f32[1]{0:T(128)} %bitcast.101), channel_id=1, replica_groups=mesh['gx'=8,'gy'=4] {'gx'}, use_global_device_ids=true, to_apply=%region_13.0 | all-reduce | flops 2 | bytes 16 | tf_op jit(solution)/shard_map/psum | solution.py:81
  1497.6 7.7 reshape.2332
  1509.5 8.6 convolution_bitcast_fusion
  1525.9 12.4 fusion.17
  1545.1 11.0 fusion.53
  1563.6 12.6 multiply_add_fusion
  1576.2 101.4 %add_multiply_fusion.1 = (f32[1,1,524288]{2,1,0:T(1,128)S(1)}, f32[1,1,524288]{2,1,0:T(1,128)S(1)}) fusion(f32[1,1,524288]{2,1,0:T(1,128)S(1)} %copy-done.5, f32[1,1,524288]{2,1,0:T(1,128)S(1)} %copy-done.3, f32[1,1,524288]{2,1,0:T(1,128)S(1)} %get-tuple-element.26, f32[1,2,524288]{2,1,0:T(2,128)S(1)} %multiply_add_fusion, f32[]{:T(128)} %bitcast.112, ...), kind=kLoop, calls=%fused_computation.90 | loop fusion | flops 95944704 | bytes 14680084 | tf_op jit(solution)/shard_map/mul | solution.py:95
  (110 shorter events, 153.9 us)
Async XLA Ops:
  0.6 282.8 %collective-permute-start = (f32[1,2,524288]{2,1,0:T(2,128)}, f32[1,2,524288]{2,1,0:T(2,128)}, u32[]{:S(2)}, u32[]{:S(2)}) collective-permute-start(f32[1,2,524288]{2,1,0:T(2,128)} %param.4), channel_id=1, source_target_pairs={{0,4},{4,0},{8,12},{12,8},{16,20},{20,16},{24,28},{28,24},{1,5},{5... | collective-permute-start | bytes 12582920 | tf_op jit(solution)/shard_map/ppermute | solution.py:11
  3.7 279.8 %collective-permute-start.2 = (f32[1,2,524288]{2,1,0:T(2,128)}, f32[1,2,524288]{2,1,0:T(2,128)}, u32[]{:S(2)}, u32[]{:S(2)}) collective-permute-start(f32[1,2,524288]{2,1,0:T(2,128)} %param.4), channel_id=1, source_target_pairs={{0,16},{4,20},{8,24},{12,28},{16,0},{20,4},{24,8},{28,12},{1,17},{... | collective-permute-start | bytes 12582920 | tf_op jit(solution)/shard_map/ppermute | solution.py:11
  6.3 277.2 %collective-permute-start.1 = (f32[1,2,524288]{2,1,0:T(2,128)}, f32[1,2,524288]{2,1,0:T(2,128)}, u32[]{:S(2)}, u32[]{:S(2)}) collective-permute-start(f32[1,2,524288]{2,1,0:T(2,128)} %param.4), channel_id=1, source_target_pairs={{0,8},{4,12},{8,0},{12,4},{16,24},{20,28},{24,16},{28,20},{1,9},{5... | collective-permute-start | bytes 12582920 | tf_op jit(solution)/shard_map/ppermute | solution.py:11
  201.3 9.8 copy-start.25
  201.3 14.4 copy-start.23
  275.2 6.9 copy-start.24
  283.5 12.4 copy-start
  440.9 98.3 %copy-start.11 = (f32[1,1,524288]{2,1,0:T(1,128)}, f32[1,1,524288]{2,1,0:T(1,128)S(1)}, u32[]{:S(2)}) copy-start(f32[1,1,524288]{2,1,0:T(1,128)S(1)} %get-tuple-element.25) | copy-start | bytes 6291460
  544.2 258.8 %collective-permute-start.5 = (f32[1,2,524288]{2,1,0:T(2,128)}, f32[1,2,524288]{2,1,0:T(2,128)}, u32[]{:S(2)}, u32[]{:S(2)}) collective-permute-start(f32[1,2,524288]{2,1,0:T(2,128)} %pad_maximum_fusion), channel_id=1, source_target_pairs={{0,16},{4,20},{8,24},{12,28},{16,0},{20,4},{24,8},{28,12},{1,17},{... | collective-permute-start | bytes 12582920 | tf_op jit(solution)/shard_map/ppermute | solution.py:11
  544.2 258.8 %collective-permute-start.4 = (f32[1,2,524288]{2,1,0:T(2,128)}, f32[1,2,524288]{2,1,0:T(2,128)}, u32[]{:S(2)}, u32[]{:S(2)}) collective-permute-start(f32[1,2,524288]{2,1,0:T(2,128)} %pad_maximum_fusion), channel_id=1, source_target_pairs={{0,8},{4,12},{8,0},{12,4},{16,24},{20,28},{24,16},{28,20},{1,9},{5... | collective-permute-start | bytes 12582920 | tf_op jit(solution)/shard_map/ppermute | solution.py:11
  544.2 258.8 %collective-permute-start.3 = (f32[1,2,524288]{2,1,0:T(2,128)}, f32[1,2,524288]{2,1,0:T(2,128)}, u32[]{:S(2)}, u32[]{:S(2)}) collective-permute-start(f32[1,2,524288]{2,1,0:T(2,128)} %pad_maximum_fusion), channel_id=1, source_target_pairs={{0,4},{4,0},{8,12},{12,8},{16,20},{20,16},{24,28},{28,24},{1,5},{5... | collective-permute-start | bytes 12582920 | tf_op jit(solution)/shard_map/ppermute | solution.py:11
  803.0 12.6 copy-start.12
  803.0 12.6 copy-start.15
  917.1 5.3 copy-start.6
  917.1 5.3 copy-start.9
  917.1 6.1 copy-start.16
  917.1 6.1 copy-start.17
  917.1 6.1 copy-start.18
  917.1 6.3 copy-start.19
  922.4 257.6 %collective-permute-start.8 = (f32[1,2,524288]{2,1,0:T(2,128)}, f32[1,2,524288]{2,1,0:T(2,128)}, u32[]{:S(2)}, u32[]{:S(2)}) collective-permute-start(f32[1,2,524288]{2,1,0:T(2,128)} %pad_maximum_fusion.1), channel_id=1, source_target_pairs={{0,16},{4,20},{8,24},{12,28},{16,0},{20,4},{24,8},{28,12},{1,17},{... | collective-permute-start | bytes 12582920 | tf_op jit(solution)/shard_map/ppermute | solution.py:11
  922.4 257.6 %collective-permute-start.7 = (f32[1,2,524288]{2,1,0:T(2,128)}, f32[1,2,524288]{2,1,0:T(2,128)}, u32[]{:S(2)}, u32[]{:S(2)}) collective-permute-start(f32[1,2,524288]{2,1,0:T(2,128)} %pad_maximum_fusion.1), channel_id=1, source_target_pairs={{0,8},{4,12},{8,0},{12,4},{16,24},{20,28},{24,16},{28,20},{1,9},{5... | collective-permute-start | bytes 12582920 | tf_op jit(solution)/shard_map/ppermute | solution.py:11
  922.5 257.6 %collective-permute-start.6 = (f32[1,2,524288]{2,1,0:T(2,128)}, f32[1,2,524288]{2,1,0:T(2,128)}, u32[]{:S(2)}, u32[]{:S(2)}) collective-permute-start(f32[1,2,524288]{2,1,0:T(2,128)} %pad_maximum_fusion.1), channel_id=1, source_target_pairs={{0,4},{4,0},{8,12},{12,8},{16,20},{20,16},{24,28},{28,24},{1,5},{5... | collective-permute-start | bytes 12582920 | tf_op jit(solution)/shard_map/ppermute | solution.py:11
  1180.0 12.6 copy-start.8
  1180.0 12.6 copy-start.10
  1294.1 7.3 copy-start.20
  1294.1 7.3 copy-start.21
  1294.1 7.3 copy-start.22
  1299.1 264.4 %collective-permute-start.11 = (f32[1,2,524288]{2,1,0:T(2,128)}, f32[1,2,524288]{2,1,0:T(2,128)}, u32[]{:S(2)}, u32[]{:S(2)}) collective-permute-start(f32[1,2,524288]{2,1,0:T(2,128)} %pad_maximum_fusion.2), channel_id=1, source_target_pairs={{0,16},{4,20},{8,24},{12,28},{16,0},{20,4},{24,8},{28,12},{1,17},{... | collective-permute-start | bytes 12582920 | tf_op jit(solution)/shard_map/ppermute | solution.py:11
  1299.2 264.4 %collective-permute-start.10 = (f32[1,2,524288]{2,1,0:T(2,128)}, f32[1,2,524288]{2,1,0:T(2,128)}, u32[]{:S(2)}, u32[]{:S(2)}) collective-permute-start(f32[1,2,524288]{2,1,0:T(2,128)} %pad_maximum_fusion.2), channel_id=1, source_target_pairs={{0,8},{4,12},{8,0},{12,4},{16,24},{20,28},{24,16},{28,20},{1,9},{5... | collective-permute-start | bytes 12582920 | tf_op jit(solution)/shard_map/ppermute | solution.py:11
  1299.2 264.3 %collective-permute-start.9 = (f32[1,2,524288]{2,1,0:T(2,128)}, f32[1,2,524288]{2,1,0:T(2,128)}, u32[]{:S(2)}, u32[]{:S(2)}) collective-permute-start(f32[1,2,524288]{2,1,0:T(2,128)} %pad_maximum_fusion.2), channel_id=1, source_target_pairs={{0,4},{4,0},{8,12},{12,8},{16,20},{20,16},{24,28},{28,24},{1,5},{5... | collective-permute-start | bytes 12582920 | tf_op jit(solution)/shard_map/ppermute | solution.py:11
  1563.5 12.6 copy-start.3
  1563.5 12.6 copy-start.5
  (6 other events, 24.1 us)
where the time goes:
time: 1690 us; the launch traced here: 1680 us
  other arithmetic  915 us (54%)
  blocking collectives  471 us (28%)
  local copies, waits for them, and re-layouts  141 us (8%)
  matrix products  131 us (8%)
    psum x4, blocking collectives, shards(): lax.psum((jnp.sum(weight, axis=1), jnp.sum(weight * occupancy[None, :], a...  466 us
    mul x4, other arithmetic, shards(): factor * (keep * real_part + time_step * coherent_real + kick * (real_par...  449 us
    reduce_sum x3, other arithmetic, shards(): jnp.sum(weight * occupancy[None, :], axis=1)  205 us
    neg x1, other arithmetic, shards(): coherent_real = -result[:, 1] - energy[None, :] * imag_part  98.3 us
    reduce_sum x1, other arithmetic, shards(): jnp.sum(weight, axis=1)  91.3 us
    dot_general x8, matrix products, block_flip(): jnp.einsum('pcakb,kj->pcajb', viewed, table, precision=lax.Precision.HIGH...  85.6 us
    reshape x8, local copies, waits for them, and re-layouts, block_flip(): return result.reshape(shape)  58.7 us
    add x4, other arithmetic, shards(): result = result + fields[low_bits + b] * from_partner(amplitudes, 'gx', b)  50.1 us
  transfers between devices with their start and end apart: 12, of which 0 were waited for; matrix products, arithmetic and copies ran while one was open for 34% of the time, Pallas kernels for 0%

commit v1 on v0

v1 whole, which is shorter than its diff:
```python
import functools

import jax
import jax.numpy as jnp
from jax import lax
from jax.experimental import pallas as pl
from jax.experimental.pallas import tpu as pltpu
from jax.sharding import PartitionSpec as P

kappa_rate = 4.0
time_step = 0.05
LANES = 128
CHUNK = 64


def bit_spin(ids, q):
    return 1.0 - 2.0 * (ids >> q & 1).astype(jnp.float32)


def step_kernel(
    high_bits, spins, table, params, block_params, fields, flips, low_energy, own, *rest
):
    partners = rest[:high_bits]
    out, sums = rest[high_bits:]
    rows = own.shape[2]
    row_bits = rows.bit_length() - 1
    chunk_bits = CHUNK.bit_length() - 1
    g = pl.program_id(0)
    rate, factor, damp, kick_one, kick_two, magnet = (params[k] for k in range(6))
    high_ones, top_link, lane_link, high_energy = (block_params[g * 4 + k] for k in range(4))

    row_ids = lax.broadcasted_iota(jnp.int32, (CHUNK, LANES), 0)
    lane_ids = lax.broadcasted_iota(jnp.int32, (CHUNK, LANES), 1)
    ones = jnp.zeros((CHUNK, LANES), jnp.int32)
    for k in range(7):
        ones = ones + (lane_ids >> k & 1)
    for k in range(chunk_bits):
        ones = ones + (row_ids >> k & 1)
    inner_ones = ones.astype(jnp.float32) * (1.0 / spins)
    lane_row = bit_spin(lax.broadcasted_iota(jnp.int32, (8, LANES), 1), 0) * lane_link
    sub = lax.broadcasted_iota(jnp.int32, (CHUNK // 8, 8, LANES), 1)
    odd = (sub & 1) == 1
    second = (sub & 2) == 2
    weights = flips[...]

    def flipped(c, j):
        base = pl.multiple_of(j * CHUNK, CHUNK)
        x = own[0, c, pl.ds(base, CHUNK), :]
        coarse = x.astype(jnp.bfloat16)
        fine = (x - coarse.astype(jnp.float32)).astype(jnp.bfloat16)
        product = jnp.dot(
            jnp.concatenate([coarse, fine], axis=1), weights, preferred_element_type=jnp.float32
        )
        total = product[:, :LANES] + product[:, LANES:]
        x3 = x.reshape(CHUNK // 8, 8, LANES)
        near = jnp.where(odd, pltpu.roll(x3, 1, 1), pltpu.roll(x3, 7, 1))
        middle = jnp.where(second, pltpu.roll(x3, 2, 1), pltpu.roll(x3, 6, 1))
        far = pltpu.roll(x3, 4, 1)
        side = fields[7] * near + fields[8] * middle + fields[9] * far
        total = total + side.reshape(CHUNK, LANES)
        for k in range(3, chunk_bits):
            size = 1 << k
            parts = [
                x[(p ^ 1) * size : ((p ^ 1) + 1) * size] for p in range(CHUNK // size)
            ]
            total = total + fields[7 + k] * jnp.concatenate(parts, axis=0)
        for k in range(chunk_bits, row_bits):
            other = pl.multiple_of((j ^ (1 << (k - chunk_bits))) * CHUNK, CHUNK)
            total = total + fields[7 + k] * own[0, c, pl.ds(other, CHUNK), :]
        for b in range(high_bits):
            total = total + fields[7 + row_bits + b] * partners[b][0, c, pl.ds(base, CHUNK), :]
        return x, total

    def body(j, carry):
        norm, tilt = carry
        base = pl.multiple_of(j * CHUNK, CHUNK)
        count = jnp.int32(0)
        for k in range(row_bits - chunk_bits):
            count = count + (j >> k & 1)
        outer_ones = count.astype(jnp.float32) * (1.0 / spins) + high_ones
        top_spin = 1 - 2 * (j >> (row_bits - chunk_bits - 1) & 1)
        constant = top_spin.astype(jnp.float32) * top_link + high_energy
        real, flip_real = flipped(0, j)
        imag, flip_imag = flipped(1, j)
        shift = inner_ones + (outer_ones - magnet)
        energy = low_energy[pl.ds(base, CHUNK), :].reshape(CHUNK // 8, 8, LANES)
        energy = (energy + (lane_row + constant)[None]).reshape(CHUNK, LANES)
        keep = factor + shift * (kick_one - damp * shift)
        turn = kick_two * shift + rate * energy
        new_real = keep * real - turn * imag - rate * flip_imag
        new_imag = keep * imag + turn * real + rate * flip_real
        out[0, 0, pl.ds(base, CHUNK), :] = new_real
        out[0, 1, pl.ds(base, CHUNK), :] = new_imag
        weight = new_real * new_real + new_imag * new_imag
        tilted = weight * (inner_ones + outer_ones)
        norm = norm + jnp.sum(weight.reshape(CHUNK // 8, 8, LANES), axis=0)
        tilt = tilt + jnp.sum(tilted.reshape(CHUNK // 8, 8, LANES), axis=0)
        return norm, tilt

    zero = jnp.zeros((8, LANES), jnp.float32)
    norm, tilt = lax.fori_loop(0, rows // CHUNK, body, (zero, zero))
    sums[0, 0] = norm
    sums[0, 1] = tilt


def one_step(blocks, table, count, params, block_params, fields, flips, low_energy, high_bits, spins):
    _, _, rows, _ = blocks.shape
    shape = (1, 2, rows, LANES)
    smem = pl.BlockSpec(memory_space=pltpu.SMEM)

    def pick(slot):
        return pl.BlockSpec(shape, lambda g, t: (t[g * (1 + high_bits) + slot], 0, 0, 0))

    grid_spec = pltpu.PrefetchScalarGridSpec(
        num_scalar_prefetch=1,
        grid=(count,),
        in_specs=[
            smem,
            smem,
            smem,
            pl.BlockSpec((2 * LANES, 2 * LANES), lambda g, t: (0, 0)),
            pl.BlockSpec((rows, LANES), lambda g, t: (0, 0)),
        ]
        + [pick(slot) for slot in range(1 + high_bits)],
        out_specs=[
            pl.BlockSpec(shape, lambda g, t: (g, 0, 0, 0)),
            pl.BlockSpec((1, 2, 8, LANES), lambda g, t: (g, 0, 0, 0)),
        ],
    )
    return pl.pallas_call(
        functools.partial(step_kernel, high_bits, spins),
        grid_spec=grid_spec,
        out_shape=[
            jax.ShapeDtypeStruct((count, 2, rows, LANES), jnp.float32),
            jax.ShapeDtypeStruct((count, 2, 8, LANES), jnp.float32),
        ],
        compiler_params=pltpu.CompilerParams(vmem_limit_bytes=58 << 20),
    )(table, params, block_params, fields, flips, low_energy, *([blocks] * (1 + high_bits)))


def shards(state, fields, couplings, noise):
    local_len = state.shape[2]
    low_bits = local_len.bit_length() - 1
    blocks_all = lax.axis_size("gx")
    high_bits = blocks_all.bit_length() - 1
    spins = low_bits + high_bits
    steps = noise.shape[1]
    rows = local_len // LANES
    me = lax.axis_index("gx")
    f32 = jnp.float32

    order = sorted(range(blocks_all), key=lambda p: (bin(p).count("1"), p))
    place = {p: g for g, p in enumerate(order)}

    x = state.reshape(2, rows, LANES)
    row_ids = lax.broadcasted_iota(jnp.int32, (rows, LANES), 0)
    lane_ids = lax.broadcasted_iota(jnp.int32, (rows, LANES), 1)
    position = row_ids * LANES + lane_ids
    low_energy = jnp.zeros((rows, LANES), f32)
    occupancy = jnp.zeros((rows, LANES), jnp.int32)
    for q in range(low_bits):
        occupancy = occupancy + (position >> q & 1)
    for q in range(low_bits - 1):
        low_energy = low_energy + couplings[q] * bit_spin(position, q) * bit_spin(position, q + 1)
    own_ones = lax.population_count(me)
    weight = x[0] * x[0] + x[1] * x[1]
    start = jnp.stack(
        [
            jnp.sum(weight),
            jnp.sum(weight * ((occupancy + own_ones).astype(f32) * (1.0 / spins))),
        ]
    )
    totals = lax.psum(start, "gx")

    ids = lax.iota(jnp.int32, LANES)
    distance = ids[:, None] ^ ids[None, :]
    lane_flip = jnp.zeros((LANES, LANES), f32)
    for q in range(7):
        lane_flip = lane_flip + fields[q] * (distance == 1 << q).astype(f32)
    coarse = lax.reduce_precision(lane_flip, 8, 7)
    fine = (lane_flip - coarse).astype(jnp.bfloat16)
    coarse = coarse.astype(jnp.bfloat16)
    flips = jnp.concatenate(
        [
            jnp.concatenate([coarse, fine], axis=1),
            jnp.concatenate([coarse, jnp.zeros_like(fine)], axis=1),
        ],
        axis=0,
    )

    targets = me ^ jnp.array(order, jnp.int32)
    high_spin = [bit_spin(targets, b) for b in range(high_bits)]
    high_energy = jnp.zeros((blocks_all,), f32)
    for b in range(high_bits - 1):
        high_energy = high_energy + couplings[low_bits + b] * high_spin[b] * high_spin[b + 1]
    block_params = jnp.stack(
        [
            lax.population_count(targets).astype(f32) * (1.0 / spins),
            couplings[low_bits - 1] * high_spin[0],
            couplings[spins - 1] * high_spin[-1],
            high_energy,
        ],
        axis=1,
    ).reshape(-1)

    blocks = lax.all_gather(x, "gx")
    half_root = jnp.sqrt(f32(time_step / 2.0))
    root_kappa = jnp.sqrt(f32(kappa_rate))
    records = []
    for s in range(steps):
        reach = steps - 1 - s
        count = sum(bin(p).count("1") <= reach for p in order)
        if blocks_all - count <= 1:
            count = blocks_all
        table = [[place[order[g]]] + [place[order[g] ^ 1 << b] for b in range(high_bits)] for g in range(count)]
        if s == 0:
            absolute = [[order[slot] for slot in entry] for entry in table]
            table = me ^ jnp.array(absolute, jnp.int32).reshape(-1)
        else:
            table = jnp.array(table, jnp.int32).reshape(-1)
        magnet = totals[1] / totals[0]
        factor = jnp.sqrt(f32(local_len * blocks_all) / totals[0])
        first = noise[0, s, 0] * half_root
        second = noise[0, s, 1] * half_root
        params = jnp.stack(
            [
                factor * time_step,
                factor,
                factor * (time_step * kappa_rate * 0.5),
                factor * root_kappa * first,
                factor * root_kappa * second,
                magnet,
            ]
        )
        drift = root_kappa * magnet * time_step
        records.append(jnp.stack([drift + first, drift + second]))
        blocks, sums = one_step(
            blocks, table, count, params, block_params, fields, flips, low_energy, high_bits, spins
        )
        if s < steps - 1:
            if count == blocks_all:
                totals = jnp.sum(sums, axis=(0, 2, 3))
            else:
                totals = lax.psum(jnp.sum(sums[0], axis=(1, 2)), "gx")
    local = jnp.where(me == 0, jnp.stack(records), 0.0)
    record = lax.psum(local, ("gx", "gy"))
    return blocks.reshape(1, 2, local_len), record


def solution(mesh):
    placed = (P("gy", None, "gx"), P(), P(), P("gy", None, None))
    return jax.shard_map(
        shards, mesh=mesh, in_specs=placed, out_specs=(P("gy", None, "gx"), P()), check_vma=False
    )
```

time: 1690 us -> 1070 us (0.63)
  other arithmetic: 915 us -> 49.3 us
  waiting for transfers between devices: 0.03 us -> 528 us
  blocking collectives: 471 us -> 110 us
  Pallas kernels: 0 us -> 325 us
  matrix products: 131 us -> 0 us
  local copies, waits for them, and re-layouts: 141 us -> 21.6 us
  between operations: 14.7 us -> 32.5 us
    all_gather x0 -> x1, waiting for transfers between devices: none -> 528 us  [shards(): blocks = lax.all_gather(x, 'gx')]
    mul x4 -> x1, other arithmetic: 449 us -> 0.01 us  [shards(): position = row_ids * LANES + lane_ids]
    psum x5 -> x3, blocking collectives: 471 us -> 110 us  [the longest x1 53.2 us: shards(): totals = lax.psum(start, 'gx')]
    pallas_call x0 -> x4, Pallas kernels: none -> 325 us  [one_step(): pl.pallas_call(functools.partial(step_kernel, high_bits, spins), grid_spe...]
    reduce_sum x4, other arithmetic: 296 us -> 13.3 us  [the longest x1 10.7 us: shards(): jnp.sum(weight)]
    dot_general x12 -> x0, matrix products: 131 us -> none  [the longest x8 85.6 us: block_flip(): jnp.einsum('pcakb,kj->pcajb', viewed, table, precision=lax.Precision.HIGH...]
    reshape x16 -> x3, local copies, waits for them, and re-layouts: 117 us -> 8.01 us  [the longest x1 6.87 us: shards(): return (blocks.reshape(1, 2, local_len), record)]
    neg x1 -> x0, other arithmetic: 98.3 us -> none  [shards(): coherent_real = -result[:, 1] - energy[None, :] * imag_part]
  transfers between devices with their start and end apart: 12 -> 1, of which waited for: 0 -> 1; matrix products, arithmetic and copies ran while one was open for 34% -> 5% of each run, Pallas kernels for 0% -> 0%
where the time goes in v1:
time: 1070 us
  waiting for transfers between devices  528 us (49%)
  Pallas kernels  325 us (30%)
  blocking collectives  110 us (10%)
  other arithmetic  49.3 us (5%)
  between operations  32.5 us (3%)
  local copies, waits for them, and re-layouts  21.6 us (2%)
    all_gather x1, waiting for transfers between devices, shards(): blocks = lax.all_gather(x, 'gx')  528 us
    pallas_call x4, Pallas kernels, one_step(): pl.pallas_call(functools.partial(step_kernel, high_bits, spins), grid_spe...  325 us
    psum x1, blocking collectives, shards(): totals = lax.psum(start, 'gx')  53.2 us
    psum x1, blocking collectives, shards(): record = lax.psum(local, ('gx', 'gy'))  36.9 us
    add x1, other arithmetic, shards(): low_energy + couplings[q] * bit_spin(position, q) * bit_spin(position, q...  23 us
  transfers between devices with their start and end apart: 1, of which 1 were waited for; matrix products, arithmetic and copies ran while one was open for 5% of the time, Pallas kernels for 0%

profile of v1, /device:TPU:0, one launch (start us, length us, event | category | flops | bytes accessed | tf_op | source)
XLA Modules:
  0.0 1066.9 jit_solution(365287216017143029)
XLA Ops:
  7.2 4.5 copy.19
  11.7 3.6 shift-right-arithmetic_and_fusion.4
  15.4 10.7 fusion.25
  26.1 1.4 pad_maximum_fusion.1
  27.5 53.2 %psum.21 = f32[2]{0:T(128)S(1)} all-reduce(f32[2]{0:T(128)S(1)} %pad_maximum_fusion.1), channel_id=1, replica_groups=mesh['gx'=8,'gy'=4] {'gx'}, use_global_device_ids=true, to_apply=%region_2.0 | all-reduce | flops 2 | bytes 16 | tf_op jit(solution)/shard_map/psum | solution.py:173
  82.1 0.7 fusion.26
  86.8 0.7 fusion.31
  87.4 0.7 fusion.30
  88.1 2.6 fusion.12
  90.9 0.7 reshape.338.block_params
  91.6 0.6 xor.65.table
  95.8 0.7 stack.150.params
  96.6 0.7 fusion.32
  97.2 4.3 reduce-precision_convert_fusion
  101.5 0.7 fusion.1.flips
  102.2 23.0 %multiply_add_fusion.low_energy = f32[4096,128]{1,0:T(8,128)} fusion(f32[]{:T(128)} %bitcast.47, f32[]{:T(128)} %bitcast.46, f32[]{:T(128)} %bitcast.45, f32[]{:T(128)} %bitcast.44, f32[]{:T(128)} %bitcast.43, f32[]{:T(128)} %bitcast.42, f32[]{:T(128)} %bitcast.41, f32[]{:T(128)} %bitcast.40, f32[]{:T(128)} %bitcast.39, f32[]{:T(128)} %bitcast.38, ...), kind=kLoop, calls=%fused_computation.2 | loop fusion | flops 78118912 | bytes 2113608 | tf_op jit(solution)/shard_map/add | solution.py:164
  125.2 527.7 %all-gather.2.cloned.1.call-done.own.rest_0_.rest_1_.rest_2_ = f32[8,2,4096,128]{3,2,1,0:T(8,128)} async-done(((f32[1,2,4096,128]{3,2,1,0:T(8,128)}), f32[8,2,4096,128]{3,2,1,0:T(8,128)}) %all-gather.2.cloned.1.call-update) | async-done | bytes 33554448 | tf_op jit(solution)/shard_map/all_gather | solution.py:206
  652.9 119.1 %shard_map.104 = (f32[8,2,4096,128]{3,2,1,0:T(8,128)}, f32[8,2,8,128]{3,2,1,0:T(8,128)}) custom-call(s32[32]{0:T(128)} %xor.65.table, f32[6]{0:T(128)} %stack.150.params, f32[32]{0:T(128)} %reshape.338.block_params, f32[22]{0:T(128)} %fields.7, bf16[256,256]{1,0:T(8,128)(2,1)} %fusion.1.flips, f32[4096,128]{1,0:T(8,128)} %multiply_add_fusion.low_energy, ...), custom_call_target="tpu_custom_call" | custom-call | tf_op jit(solution)/shard_map/pallas_call | solution.py:130
  772.0 0.9 reduce_sum.47
  772.9 0.6 fusion.29
  776.7 0.7 stack.160.params
  777.4 119.1 %shard_map.105 = (f32[8,2,4096,128]{3,2,1,0:T(8,128)}, f32[8,2,8,128]{3,2,1,0:T(8,128)}) custom-call(s32[32]{0:T(128)} %constant.131.table, f32[6]{0:T(128)} %stack.160.params, f32[32]{0:T(128)} %reshape.338.block_params, f32[22]{0:T(128)} %fields.7, bf16[256,256]{1,0:T(8,128)(2,1)} %fusion.1.flips, f32[4096,128]{1,0:T(8,128)} %multiply_add_fusion.low_energy, ...), custom_call_target="tpu_custom_call" | custom-call | tf_op jit(solution)/shard_map/pallas_call | solution.py:130
  896.5 0.9 reduce_sum.48
  901.3 0.7 stack.165.params
  902.0 64.7 %shard_map.106 = (f32[4,2,4096,128]{3,2,1,0:T(8,128)}, f32[4,2,8,128]{3,2,1,0:T(8,128)}) custom-call(s32[16]{0:T(128)} %constant.130.table, f32[6]{0:T(128)} %stack.165.params, f32[32]{0:T(128)} %reshape.338.block_params, f32[22]{0:T(128)} %fields.7, bf16[256,256]{1,0:T(8,128)(2,1)} %fusion.1.flips, f32[4096,128]{1,0:T(8,128)} %multiply_add_fusion.low_energy, ...), custom_call_target="tpu_custom_call" | custom-call | tf_op jit(solution)/shard_map/pallas_call | solution.py:130
  966.7 0.8 slice_reduce_fusion
  967.5 20.2 %psum.22 = f32[2]{0:T(128)S(1)} all-reduce(f32[2]{0:T(128)S(1)} %slice_reduce_fusion), channel_id=1, replica_groups=mesh['gx'=8,'gy'=4] {'gx'}, use_global_device_ids=true, to_apply=%region_6.0 | all-reduce | flops 2 | bytes 16 | tf_op jit(solution)/shard_map/psum | solution.py:244
  991.8 36.9 %psum.23 = f32[4,2]{1,0:T(4,128)S(1)} all-reduce(f32[4,2]{1,0:T(4,128)S(1)} %maximum_select_fusion), channel_id=1, replica_groups=mesh['gx'=8,'gy'=4] {'gx','gy'}, use_global_device_ids=true, to_apply=%region_7.8 | all-reduce | flops 8 | bytes 64 | tf_op jit(solution)/shard_map/psum | solution.py:246
  1028.8 0.6 copy.16
  1029.4 0.7 stack.170.params
  1030.6 22.6 %shard_map.107 = (f32[1,2,4096,128]{3,2,1,0:T(8,128)}, f32[1,2,8,128]{3,2,1,0:T(8,128)}) custom-call(s32[4]{0:T(128)} %iota.239.table, f32[6]{0:T(128)} %stack.170.params, f32[32]{0:T(128)} %reshape.338.block_params, f32[22]{0:T(128)} %fields.7, bf16[256,256]{1,0:T(8,128)(2,1)} %fusion.1.flips, f32[4096,128]{1,0:T(8,128)} %multiply_add_fusion.low_energy, ...), custom_call_target="tpu_custom_call" | custom-call | tf_op jit(solution)/shard_map/pallas_call | solution.py:130
  1053.2 6.9 reshape.339
  (27 shorter events, 2.7 us)
Async XLA Ops:
  7.2 645.7 %all-gather.2.cloned.1.call-start = ((), (), s32[]{:S(2)}) async-start(), calls=%async_computation | async-start | bytes 37748736 | tf_op jit(solution)/shard_map/all_gather | solution.py:206
  11.7 3.6 copy-start
  15.4 66.7 %copy-start.3 = (f32[1,4,2]{1,2,0:T(2,128)S(1)}, f32[1,4,2]{1,2,0:T(2,128)}, u32[]{:S(2)}) copy-start(f32[1,4,2]{1,2,0:T(2,128)} %param.12) | copy-start | bytes 100
  15.4 71.3 %copy-start.1 = (f32[22]{0:T(128)S(1)}, f32[22]{0:T(128)}, u32[]{:S(2)}) copy-start(f32[22]{0:T(128)} %param.11) | copy-start | bytes 268
  15.4 72.7 %copy-start.5 = (s32[8]{0:T(128)S(1)}, s32[8]{0:T(128)}, u32[]{:S(2)}) copy-start(s32[8]{0:T(128)} %constant.120.clone) | copy-start | bytes 100
  15.4 76.1 %copy-start.4 = (s32[8,4]{1,0:T(8,128)S(1)}, s32[8,4]{1,0:T(8,128)}, u32[]{:S(2)}) copy-start(s32[8,4]{1,0:T(8,128)} %constant.121.clone) | copy-start | bytes 388
  15.4 81.1 %copy-start.2 = (f32[22]{0:T(128)S(1)}, f32[22]{0:T(128)}, u32[]{:S(2)}) copy-start(f32[22]{0:T(128)} %fields.7) | copy-start | bytes 268
Sparse Core Ops, SparseCore 0:
  11.8 640.9 all-gather.1

commit v2 on v1

--- a/solution.py
+++ b/solution.py
@@ -203,7 +203,26 @@
         axis=1,
     ).reshape(-1)
 
-    blocks = lax.all_gather(x, "gx")
+    ring = list(range(0, blocks_all, 2)) + list(range(blocks_all - 1, 0, -2))
+    ahead = [(ring[i - 1], ring[i]) for i in range(blocks_all)]
+    back = [(target, source) for source, target in ahead]
+    half = blocks_all // 2
+    slots = [None] * blocks_all
+    slots[0] = x
+    from_back = from_ahead = x
+    for hop in range(1, half):
+        from_back = lax.ppermute(from_back, "gx", ahead)
+        from_ahead = lax.ppermute(from_ahead, "gx", back)
+        slots[hop] = from_back
+        slots[blocks_all - hop] = from_ahead
+    slots[half] = jnp.concatenate(
+        [lax.ppermute(from_back[:1], "gx", ahead), lax.ppermute(from_ahead[1:], "gx", back)]
+    )
+    blocks = jnp.stack(slots)
+
+    def ring_place(i):
+        return jnp.where(i & 1 == 1, blocks_all - 1 - (i >> 1), i >> 1)
+
     half_root = jnp.sqrt(f32(time_step / 2.0))
     root_kappa = jnp.sqrt(f32(kappa_rate))
     records = []
@@ -215,7 +234,8 @@
         table = [[place[order[g]]] + [place[order[g] ^ 1 << b] for b in range(high_bits)] for g in range(count)]
         if s == 0:
             absolute = [[order[slot] for slot in entry] for entry in table]
-            table = me ^ jnp.array(absolute, jnp.int32).reshape(-1)
+            target = me ^ jnp.array(absolute, jnp.int32).reshape(-1)
+            table = (ring_place(me) - ring_place(target)) & (blocks_all - 1)
         else:
             table = jnp.array(table, jnp.int32).reshape(-1)
         magnet = totals[1] / totals[0]

time: 1070 us -> 768 us (0.72)
  waiting for transfers between devices: 528 us -> 165 us
  blocking collectives: 110 us -> 144 us
  local copies, waits for them, and re-layouts: 21.6 us -> 51.2 us
  between operations: 32.5 us -> 18.9 us
    all_gather x1 -> x0, waiting for transfers between devices: 528 us -> none  [shards(): blocks = lax.all_gather(x, 'gx')]
    ppermute x0 -> x8, waiting for transfers between devices: none -> 165 us  [the longest x3 134 us: shards(): from_back = lax.ppermute(from_back, 'gx', ahead)]
    psum x1, blocking collectives: 53.2 us -> 88.5 us  [shards(): totals = lax.psum(start, 'gx')]
    unnamed x14 -> x18, local copies, waits for them, and re-layouts: 5.16 us -> 22.8 us
  transfers between devices with their start and end apart: 1 -> 8, of which waited for: 1 -> 4; matrix products, arithmetic and copies ran while one was open for 5% -> 9% of each run, Pallas kernels for 0% -> 0%
where the time goes in v2:
time: 768 us; the launch traced here: 766 us
  Pallas kernels  325 us (42%)
  waiting for transfers between devices  165 us (21%)
  blocking collectives  144 us (19%)
  other arithmetic  52.4 us (7%)
  local copies, waits for them, and re-layouts  51.2 us (7%)
  between operations  18.9 us (2%)
  starting transfers between devices  9.26 us (1%)
    pallas_call x4, Pallas kernels, one_step(): pl.pallas_call(functools.partial(step_kernel, high_bits, spins), grid_spe...  325 us
    ppermute x3, waiting for transfers between devices, shards(): from_back = lax.ppermute(from_back, 'gx', ahead)  134 us
    psum x1, blocking collectives, shards(): totals = lax.psum(start, 'gx')  88.5 us
    psum x1, blocking collectives, shards(): record = lax.psum(local, ('gx', 'gy'))  37.1 us
    ppermute x1, waiting for transfers between devices, shards(): lax.ppermute(from_back[:1], 'gx', ahead)  29.6 us
    add x1, other arithmetic, shards(): low_energy + couplings[q] * bit_spin(position, q) * bit_spin(position, q...  23.3 us
    unnamed x18, local copies, waits for them, and re-layouts  22.8 us
    psum x1, blocking collectives, shards(): totals = lax.psum(jnp.sum(sums[0], axis=(1, 2)), 'gx')  18.6 us
  transfers between devices with their start and end apart: 8, of which 4 were waited for; matrix products, arithmetic and copies ran while one was open for 9% of the time, Pallas kernels for 0%

profile of v2, /device:TPU:0, one launch (start us, length us, event | category | flops | bytes accessed | tf_op | source)
XLA Modules:
  0.0 765.8 jit_solution(5326937247487450440)
XLA Ops:
  0.6 4.7 copy_bitcast_fusion
  5.3 3.1 collective-permute-start
  8.4 90.6 %collective-permute-done = f32[2,4096,128]{2,1,0:T(8,128)} collective-permute-done((f32[2,4096,128]{2,1,0:T(8,128)S(1)}, f32[2,4096,128]{2,1,0:T(8,128)}, u32[]{:S(2)}, u32[]{:S(2)}) %collective-permute-start) | collective-permute-done | bytes 4194336 | tf_op jit(solution)/shard_map/ppermute | solution.py:214
  99.0 1.8 collective-permute-start.1
  101.0 3.6 shift-right-arithmetic_and_fusion.4
  104.7 10.6 %fusion.29 = (f32[]{:T(128)}, f32[]{:T(128)}) fusion(s32[]{:T(128)S(6)} %population_count.6, s32[1,1,524288]{2,1,0:T(1,128)S(1)} %bitcast.122, s32[1,1,524288]{2,1,0:T(1,128)S(1)} %bitcast.123, s32[1,1,524288]{2,1,0:T(1,128)S(1)} %bitcast.124, s32[1,1,524288]{2,1,0:T(1,128)S(1)} %bitcast.125, s32[1,1,524288]{2,1,0:T(1,128)S(1)} %bitcast.126, ...), kind=kLoop, calls=%fused_computation.86 | loop fusion | flops 7340030 | bytes 16777228 | tf_op jit(solution)/shard_map/reduce_sum | solution.py:169
  115.3 1.4 pad_maximum_fusion.1
  116.6 88.5 %psum.21 = f32[2]{0:T(128)S(1)} all-reduce(f32[2]{0:T(128)S(1)} %pad_maximum_fusion.1), channel_id=1, replica_groups=mesh['gx'=8,'gy'=4] {'gx'}, use_global_device_ids=true, to_apply=%region_2.0 | all-reduce | flops 2 | bytes 16 | tf_op jit(solution)/shard_map/psum | solution.py:173
  207.9 2.6 fusion.14
  210.5 2.0 collective-permute-start.6
  223.1 4.5 reduce-precision_convert_fusion
  228.7 23.3 %multiply_add_fusion.low_energy = f32[4096,128]{1,0:T(8,128)} fusion(f32[]{:T(128)} %bitcast.47, f32[]{:T(128)} %bitcast.46, f32[]{:T(128)} %bitcast.45, f32[]{:T(128)} %bitcast.44, f32[]{:T(128)} %bitcast.43, f32[]{:T(128)} %bitcast.42, f32[]{:T(128)} %bitcast.41, f32[]{:T(128)} %bitcast.40, f32[]{:T(128)} %bitcast.39, f32[]{:T(128)} %bitcast.38, ...), kind=kLoop, calls=%fused_computation.11 | loop fusion | flops 78118912 | bytes 2113608 | tf_op jit(solution)/shard_map/add | solution.py:164
  252.1 4.4 bitcast_dynamic-update-slice_fusion.6
  256.5 43.1 %collective-permute-done.2 = f32[2,4096,128]{2,1,0:T(8,128)} collective-permute-done((f32[2,4096,128]{2,1,0:T(8,128)}, f32[2,4096,128]{2,1,0:T(8,128)}, u32[]{:S(2)}, u32[]{:S(2)}) %collective-permute-start.2) | collective-permute-done | bytes 4194336 | tf_op jit(solution)/shard_map/ppermute | solution.py:214
  299.7 1.7 slice.208
  301.5 1.7 slice.209
  303.2 2.1 collective-permute-start.7
  305.3 4.4 bitcast_dynamic-update-slice_fusion.5
  309.7 4.4 bitcast_dynamic-update-slice_fusion.4
  314.1 29.6 %collective-permute-done.3 = f32[1,4096,128]{2,1,0:T(8,128)S(1)} collective-permute-done((f32[1,4096,128]{2,1,0:T(8,128)S(1)}, f32[1,4096,128]{2,1,0:T(8,128)S(1)}, u32[]{:S(2)}, u32[]{:S(2)}) %collective-permute-start.3) | collective-permute-done | bytes 2097184 | tf_op jit(solution)/shard_map/ppermute | solution.py:219
  343.7 1.2 collective-permute-done.7
  344.9 2.2 fusion
  347.1 4.4 bitcast_dynamic-update-slice_fusion.3
  351.5 4.4 bitcast_dynamic-update-slice_fusion.2
  355.9 4.4 bitcast_dynamic-update-slice_fusion.1.own.rest_0_.rest_1_.rest_2_
  360.3 119.1 %shard_map.104 = (f32[8,2,4096,128]{3,2,1,0:T(8,128)}, f32[8,2,8,128]{3,2,1,0:T(8,128)}) custom-call(s32[32]{0:T(128)} %fusion.28.table, f32[6]{0:T(128)} %stack.174.params, f32[32]{0:T(128)} %reshape.346.block_params, f32[22]{0:T(128)} %fields.7, bf16[256,256]{1,0:T(8,128)(2,1)} %fusion.2.flips, f32[4096,128]{1,0:T(8,128)} %multiply_add_fusion.low_energy, ...), custom_call_target="tpu_custom_call" | custom-call | tf_op jit(solution)/shard_map/pallas_call | solution.py:130
  484.7 119.0 %shard_map.105 = (f32[8,2,4096,128]{3,2,1,0:T(8,128)}, f32[8,2,8,128]{3,2,1,0:T(8,128)}) custom-call(s32[32]{0:T(128)} %constant.135.table, f32[6]{0:T(128)} %stack.192.params, f32[32]{0:T(128)} %reshape.346.block_params, f32[22]{0:T(128)} %fields.7, bf16[256,256]{1,0:T(8,128)(2,1)} %fusion.2.flips, f32[4096,128]{1,0:T(8,128)} %multiply_add_fusion.low_energy, ...), custom_call_target="tpu_custom_call" | custom-call | tf_op jit(solution)/shard_map/pallas_call | solution.py:130
  609.2 64.7 %shard_map.106 = (f32[4,2,4096,128]{3,2,1,0:T(8,128)}, f32[4,2,8,128]{3,2,1,0:T(8,128)}) custom-call(s32[16]{0:T(128)} %constant.134.table, f32[6]{0:T(128)} %stack.197.params, f32[32]{0:T(128)} %reshape.346.block_params, f32[22]{0:T(128)} %fields.7, bf16[256,256]{1,0:T(8,128)(2,1)} %fusion.2.flips, f32[4096,128]{1,0:T(8,128)} %multiply_add_fusion.low_energy, ...), custom_call_target="tpu_custom_call" | custom-call | tf_op jit(solution)/shard_map/pallas_call | solution.py:130
  674.6 18.6 %psum.22 = f32[2]{0:T(128)S(1)} all-reduce(f32[2]{0:T(128)S(1)} %slice_reduce_fusion), channel_id=1, replica_groups=mesh['gx'=8,'gy'=4] {'gx'}, use_global_device_ids=true, to_apply=%region_6.7 | all-reduce | flops 2 | bytes 16 | tf_op jit(solution)/shard_map/psum | solution.py:264
  697.4 37.1 %psum.23 = f32[4,2]{1,0:T(4,128)S(1)} all-reduce(f32[4,2]{1,0:T(4,128)S(1)} %maximum_select_fusion), channel_id=1, replica_groups=mesh['gx'=8,'gy'=4] {'gx','gy'}, use_global_device_ids=true, to_apply=%region_7.8 | all-reduce | flops 8 | bytes 64 | tf_op jit(solution)/shard_map/psum | solution.py:266
  736.3 22.6 %shard_map.107 = (f32[1,2,4096,128]{3,2,1,0:T(8,128)}, f32[1,2,8,128]{3,2,1,0:T(8,128)}) custom-call(s32[4]{0:T(128)} %iota.239.table, f32[6]{0:T(128)} %stack.202.params, f32[32]{0:T(128)} %reshape.346.block_params, f32[22]{0:T(128)} %fields.7, bf16[256,256]{1,0:T(8,128)(2,1)} %fusion.2.flips, f32[4096,128]{1,0:T(8,128)} %multiply_add_fusion.low_energy, ...), custom_call_target="tpu_custom_call" | custom-call | tf_op jit(solution)/shard_map/pallas_call | solution.py:130
  758.9 6.9 reshape.348
  (52 shorter events, 14.2 us)
Async XLA Ops:
  5.3 93.7 %collective-permute-start = (f32[2,4096,128]{2,1,0:T(8,128)S(1)}, f32[2,4096,128]{2,1,0:T(8,128)}, u32[]{:S(2)}, u32[]{:S(2)}) collective-permute-start(f32[2,4096,128]{2,1,0:T(8,128)S(1)} %get-tuple-element.22), channel_id=1, source_target_pairs={{4,0},{0,8},{8,16},{16,24},{24,28},{28,20},{20,12},{12,4},{5,1},{1... | collective-permute-start | bytes 12582920 | tf_op jit(solution)/shard_map/ppermute | solution.py:214
  8.4 92.4 %collective-permute-start.4 = (f32[2,4096,128]{2,1,0:T(8,128)S(1)}, f32[2,4096,128]{2,1,0:T(8,128)}, u32[]{:S(2)}, u32[]{:S(2)}) collective-permute-start(f32[2,4096,128]{2,1,0:T(8,128)S(1)} %get-tuple-element.22), channel_id=1, source_target_pairs={{0,4},{8,0},{16,8},{24,16},{28,24},{20,28},{12,20},{4,12},{1,5},{9... | collective-permute-start | bytes 12582920 | tf_op jit(solution)/shard_map/ppermute | solution.py:215
  99.0 111.5 %collective-permute-start.1 = (f32[2,4096,128]{2,1,0:T(8,128)}, f32[2,4096,128]{2,1,0:T(8,128)}, u32[]{:S(2)}, u32[]{:S(2)}) collective-permute-start(f32[2,4096,128]{2,1,0:T(8,128)} %collective-permute-done), channel_id=1, source_target_pairs={{4,0},{0,8},{8,16},{16,24},{24,28},{28,20},{20,12},{12,4},{5,1},{1... | collective-permute-start | bytes 12582920 | tf_op jit(solution)/shard_map/ppermute | solution.py:214
  100.8 109.8 %collective-permute-start.5 = (f32[2,4096,128]{2,1,0:T(8,128)}, f32[2,4096,128]{2,1,0:T(8,128)}, u32[]{:S(2)}, u32[]{:S(2)}) collective-permute-start(f32[2,4096,128]{2,1,0:T(8,128)} %collective-permute-done.4), channel_id=1, source_target_pairs={{0,4},{8,0},{16,8},{24,16},{28,24},{20,28},{12,20},{4,12},{1,5},{9... | collective-permute-start | bytes 12582920 | tf_op jit(solution)/shard_map/ppermute | solution.py:215
  101.0 3.6 copy-start
  104.6 101.9 %copy-start.1 = (f32[22]{0:T(128)S(1)}, f32[22]{0:T(128)}, u32[]{:S(2)}) copy-start(f32[22]{0:T(128)} %param.11) | copy-start | bytes 268
  104.6 103.2 %copy-start.5 = (s32[8]{0:T(128)S(1)}, s32[8]{0:T(128)}, u32[]{:S(2)}) copy-start(s32[8]{0:T(128)} %constant.124.clone) | copy-start | bytes 100
  104.7 107.9 %copy-start.4 = (f32[1,4,2]{1,2,0:T(2,128)S(1)}, f32[1,4,2]{1,2,0:T(2,128)}, u32[]{:S(2)}) copy-start(f32[1,4,2]{1,2,0:T(2,128)} %param.12) | copy-start | bytes 100
  104.7 113.0 %copy-start.3 = (s32[8,4]{1,0:T(8,128)S(1)}, s32[8,4]{1,0:T(8,128)}, u32[]{:S(2)}) copy-start(s32[8,4]{1,0:T(8,128)} %constant.125.clone) | copy-start | bytes 388
  104.7 117.7 %copy-start.2 = (f32[22]{0:T(128)S(1)}, f32[22]{0:T(128)}, u32[]{:S(2)}) copy-start(f32[22]{0:T(128)} %fields.7) | copy-start | bytes 268
  210.5 89.2 %collective-permute-start.2 = (f32[2,4096,128]{2,1,0:T(8,128)}, f32[2,4096,128]{2,1,0:T(8,128)}, u32[]{:S(2)}, u32[]{:S(2)}) collective-permute-start(f32[2,4096,128]{2,1,0:T(8,128)} %collective-permute-done.1), channel_id=1, source_target_pairs={{4,0},{0,8},{8,16},{16,24},{24,28},{28,20},{20,12},{12,4},{5,1},{1... | collective-permute-start | bytes 12582920 | tf_op jit(solution)/shard_map/ppermute | solution.py:214
  210.5 90.9 %collective-permute-start.6 = (f32[2,4096,128]{2,1,0:T(8,128)}, f32[2,4096,128]{2,1,0:T(8,128)}, u32[]{:S(2)}, u32[]{:S(2)}) collective-permute-start(f32[2,4096,128]{2,1,0:T(8,128)} %collective-permute-done.5), channel_id=1, source_target_pairs={{0,4},{8,0},{16,8},{24,16},{28,24},{20,28},{12,20},{4,12},{1,5},{9... | collective-permute-start | bytes 12582920 | tf_op jit(solution)/shard_map/ppermute | solution.py:215
  301.4 42.2 %collective-permute-start.3 = (f32[1,4096,128]{2,1,0:T(8,128)S(1)}, f32[1,4096,128]{2,1,0:T(8,128)S(1)}, u32[]{:S(2)}, u32[]{:S(2)}) collective-permute-start(f32[1,4096,128]{2,1,0:T(8,128)S(1)} %slice.208), channel_id=1, source_target_pairs={{4,0},{0,8},{8,16},{16,24},{24,28},{28,20},{20,12},{12,4},{5,1},{1... | collective-permute-start | bytes 6291464 | tf_op jit(solution)/shard_map/ppermute | solution.py:219
  303.2 41.6 %collective-permute-start.7 = (f32[1,4096,128]{2,1,0:T(8,128)S(1)}, f32[1,4096,128]{2,1,0:T(8,128)S(1)}, u32[]{:S(2)}, u32[]{:S(2)}) collective-permute-start(f32[1,4096,128]{2,1,0:T(8,128)S(1)} %slice.209), channel_id=1, source_target_pairs={{0,4},{8,0},{16,8},{24,16},{28,24},{20,28},{12,20},{4,12},{1,5},{9... | collective-permute-start | bytes 6291464 | tf_op jit(solution)/shard_map/ppermute | solution.py:219
